TPU v7x, 32 devices: a whole 2x2x4 slice. The times are simulated.
32 devices in a mesh: gx: 8 (over z, y), gy: 4 (over x, core).
Axes of the slice: x: 2, y: 2, z: 4, core: 2. Of those that a mesh axis runs over, the one named last changes fastest.
Arguments:
- snapshots: bfloat16 [8, 8, 4, 2048, 512], P('gx', 'gy'), may hold values from -120 to 120
- basis: bfloat16 [8, 8, 4, 24, 2048], P('gx', 'gy'), may hold values from -0.0625 to 0.0625
- node_counts: int32 [8, 8], P('gx', 'gy'), may hold values from 1024 to 2048, as said below
- adjacency: int32 [8, 8, 3], P('gx', 'gy'), may hold values from 0 to 63, as said below
Outputs:
- operator: float32 [8, 8, 397, 24], P('gx', 'gy')
- reduced_states: float32 [8, 8, 24, 512], P('gx', 'gy')
Inputs may be any that keep to these rules, and one draw needn't show every extreme that they name: Node slot n of subdomain g is live iff n < node_counts[g]; at least 1024 slots are live, and one subdomain has all 2048 live. Subdomain (row, col) has id row * 8 + col. Each row of adjacency holds 3 distinct ids other than its own subdomain's, each within one subdomain row and one subdomain column of it.
All inputs are finite; a program needn't handle non-finite values.
Results may differ from a plain program's by a relative error of at most 0.0003.
Values sent between devices are 32-bit elements; how exact they have to be, the bound alone decides.
A program may use at most 64 MiB of HBM per device.

v0:
```python
import jax
import jax.numpy as jnp
from jax import lax
from jax.sharding import PartitionSpec as P

beta_linear = 0.5
beta_quad = 0.5


def padded_2(cells, sides, width):
    for axis, dim in sides:
        count = lax.axis_size(axis)
        ends = count - 1
        head = lax.slice_in_dim(cells, 0, width, axis=dim)
        tail = lax.slice_in_dim(cells, cells.shape[dim] - width, cells.shape[dim], axis=dim)
        cells = jnp.concatenate(
            [
                lax.ppermute(tail, axis, [(i, (i + 1) % count) for i in range(ends)]),
                cells,
                lax.ppermute(head, axis, [((i + 1) % count, i) for i in range(ends)]),
            ],
            axis=dim,
        )
    return cells


def build_features(state, near):
    ranks = state.shape[1]
    steps = state.shape[2]
    pieces = [
        jnp.ones((state.shape[0], 1, steps), jnp.float32),
        state,
        near.reshape(state.shape[0], -1, steps),
    ]
    for first in range(ranks):
        pieces.append(state[:, first : first + 1] * state[:, first:])
    return jnp.concatenate(pieces, axis=1)


def pick_rows(pieces, links):
    ids = jnp.arange(pieces.shape[0], dtype=jnp.int32)
    hits = (links[:, :, None] == ids[None, None, :]).astype(jnp.float32)
    return jnp.einsum("sbn,nrk->sbrk", hits, pieces, precision=lax.Precision.HIGHEST)


def solve_one(gram, rhs):
    factor = jnp.linalg.cholesky(gram)
    middle = jax.scipy.linalg.solve_triangular(factor, rhs, lower=True)
    return jax.scipy.linalg.solve_triangular(factor, middle, lower=True, trans=1)


def body(snapshots, basis, node_counts, adjacency):
    values = snapshots[0]
    modes = basis[0]
    counts = node_counts[0]
    links = adjacency[0]
    columns = values.shape[0]
    slots = values.shape[2]
    steps = values.shape[3]
    ranks = modes.shape[2]
    live = jnp.arange(slots, dtype=jnp.int32)[None, :] < counts[:, None]
    masked = modes * live.astype(jnp.bfloat16)[:, None, None, :]
    proj = jnp.einsum("svrp,svpk->svrk", masked, values, preferred_element_type=jnp.float32)
    slotsq = jnp.einsum("svpk,svpk->svp", values, values, preferred_element_type=jnp.float32)
    squares = jnp.sum(slotsq * live.astype(jnp.float32)[:, None, :], axis=(0, 2))
    nodes = jnp.sum(counts.astype(jnp.float32))
    total_subs = lax.axis_size("gx") * lax.axis_size("gy") * columns
    grid_cols = columns * lax.axis_size("gy")
    near_row = links // grid_cols
    near_col = links % grid_cols
    local = (near_row - lax.axis_index("gx") + 1) * (columns + 2) + (
        near_col - lax.axis_index("gy") * columns + 1
    )
    cross = jnp.einsum("svrk,swrk->vw", proj, proj, precision=lax.Precision.HIGHEST)
    sq_all, nodes_all, cross_all = lax.psum((squares, nodes, cross), ("gx", "gy"))
    scale = jnp.sqrt(sq_all / (nodes_all * steps) + 1e-06)
    states = jnp.sum(proj / scale[None, :, None, None], axis=1)
    gnorm = jnp.sum(cross_all / (scale[:, None] * scale[None, :])) / (total_subs * ranks * steps)
    padded = padded_2(states[None], (("gx", 0), ("gy", 1)), 1)
    flat = padded.reshape(-1, ranks, steps)
    near = pick_rows(flat, local)
    nbrs = links.shape[1]
    feats = build_features(states, near)
    past = feats[:, :, :-1]
    nlin = 1 + ranks + nbrs * ranks
    nquad = ranks * (ranks + 1) // 2
    reg_diag = steps * jnp.concatenate(
        [
            jnp.full((nlin,), beta_linear, jnp.float32) * gnorm,
            jnp.full((nquad,), beta_quad, jnp.float32) * gnorm * gnorm,
        ]
    )
    gram = (
        jnp.einsum("sfk,sgk->sfg", past, past, precision=lax.Precision.HIGHEST)
        + jnp.diag(reg_diag)[None]
    )
    rhs = jnp.einsum("sfk,srk->sfr", past, states[:, :, 1:], precision=lax.Precision.HIGHEST)
    operator = jax.vmap(solve_one)(gram, rhs)
    return (operator[None], states[None])


def solution(mesh):
    in_specs = (
        P("gx", "gy", None, None, None),
        P("gx", "gy", None, None, None),
        P("gx", "gy"),
        P("gx", "gy", None),
    )
    out_specs = (P("gx", "gy", None, None), P("gx", "gy", None, None))
    return jax.shard_map(body, mesh=mesh, in_specs=in_specs, out_specs=out_specs, check_vma=False)
```

profile of v0, /device:TPU:1, one launch (start us, length us, event | category | flops | bytes accessed | tf_op | source)
XLA Modules:
  0.0 338.5 jit_solution(2032630812765545449)
XLA Ops:
  0.6 0.7 fusion.58
  1.4 7.5 %fusion = f32[2,4,2048]{2,1,0:T(4,128)S(1)} fusion(bf16[1,2,4,2048,512]{4,3,2,1,0:T(8,128)(2,1)} %param.4), kind=kLoop, calls=%fused_computation.3 | loop fusion | flops 25149440 | bytes 16842752 | tf_op jit(solution)/shard_map/svpk,svpk->svp/dot_general | solution.py:64
  8.9 3.2 copy-done
  12.0 3.4 %fusion.1 = f32[2,4,24,512]{3,2,1,0:T(8,128)S(1)} fusion(bf16[1,2,4,2048,512]{4,3,2,1,0:T(8,128)(2,1)S(1)} %copy-done, bf16[1,2,4,24,2048]{4,3,2,1,0:T(8,128)(2,1)} %param.5, bf16[2,2048]{1,0:T(2,128)(2,1)S(1)} %get-tuple-element.61), kind=kOutput, calls=%fused_computation.4 | convolution fusion | flops 403046400 | bytes 17965056 | tf_op jit(solution)/shard_map/svrp,svpk->svrk/dot_general | solution.py:63
  15.5 1.9 convolution_bitcast_fusion
  17.5 0.6 convert_reduce_fusion
  18.1 40.9 %all-reduce.4 = (f32[4]{0:T(128)S(1)}, f32[]{:T(128)}, f32[4,4]{1,0:T(4,128)S(1)}) all-reduce(f32[4]{0:T(128)S(1)} %multiply_reduce_fusion, f32[]{:T(128)} %convert_reduce_fusion, f32[4,4]{1,0:T(4,128)S(1)} %convolution_bitcast_fusion), channel_id=1, replica_groups=mesh['gx'=8,'gy'=4] {'gx','gy'}, use_global_device_ids=true, to_apply=%region_1.0 | all-reduce | flops 21 | bytes 168 | tf_op jit(solution)/shard_map/psum | solution.py:75
  59.8 1.3 collective-permute-start.1
  61.1 4.0 %collective-permute-start = (f32[1,2,24,512]{3,2,1,0:T(8,128)S(1)}, f32[1,2,24,512]{3,2,1,0:T(8,128)S(1)}, u32[]{:S(2)}, u32[]{:S(2)}) collective-permute-start(f32[1,2,24,512]{3,2,1,0:T(8,128)S(1)} %bitcast.156), channel_id=1, source_target_pairs={{0,4},{4,8},{8,12},{12,16},{16,20},{20,24},{24,28},{1,5},{5,9},{9,... | collective-permute-start | bytes 294920 | tf_op jit(solution)/shard_map/ppermute | solution.py:18
  65.1 0.6 iota_compare_fusion.4
  65.8 0.7 slice_multiply_fusion.22
  66.4 0.6 pad_convert_fusion
  67.1 0.8 fusion.65
  69.9 0.6 slice_multiply_fusion.21
  70.5 0.6 slice_multiply_fusion.20
  71.1 0.6 slice_multiply_fusion.19
  71.7 0.6 slice_multiply_fusion.18
  72.4 0.6 slice_multiply_fusion.16
  73.0 0.6 slice_multiply_fusion.17
  73.6 0.6 slice_multiply_fusion.15
  74.7 1.4 fusion.9
  76.1 0.6 iota_compare_fusion.8
  76.7 5.7 %collective-permute-start.2 = (f32[3,1,24,512]{3,2,1,0:T(8,128)S(1)}, f32[3,1,24,512]{3,2,1,0:T(8,128)S(1)}, u32[]{:S(2)}, u32[]{:S(2)}) collective-permute-start(f32[3,1,24,512]{3,2,1,0:T(8,128)S(1)} %get-tuple-element.26), channel_id=1, source_target_pairs={{0,1},{1,2},{2,3},{4,5},{5,6},{6,7},{8,9},{9,10},{10,11},{12,13},{... | collective-permute-start | bytes 442376 | tf_op jit(solution)/shard_map/ppermute | solution.py:18
  82.4 2.4 collective-permute-start.3
  84.8 0.6 iota_multiply_fusion
  85.4 0.8 iota_compare_fusion.2
  86.1 2.7 collective-permute-done.3
  88.9 0.8 fusion.11
  89.8 8.0 %concatenate.48 = f32[2,397,512]{2,1,0:T(8,128)S(1)} concatenate(f32[2,1,512]{2,1,0:T(1,128)S(1)} %broadcast_in_dim.45, f32[2,24,512]{2,1,0:T(8,128)S(1)} %divide_reduce_fusion, f32[2,72,512]{2,1,0:T(8,128)S(1)} %bitcast.161, f32[2,24,512]{2,1,0:T(8,128)S(1)} %broadcast_multiply_fusion, f32[2,23,512]{2,1,0:T(8,128)S(1)} %slice_multiply_fusion.6, ...), dimensions={1} | concatenate | bytes 3252224 | tf_op jit(solution)/shard_map/concatenate | solution.py:37
  97.8 1.5 fusion.5
  99.3 2.8 fusion.7
  102.2 0.7 copy.49
  102.9 2.0 fusion.4
  104.9 1.2 copy-done.2
  106.1 23.5 %custom-call.38 = f32[2,128,128]{2,1,0:T(8,128)S(1)} custom-call(f32[2,128,128]{2,1,0:T(8,128)S(1)} %cholesky.281), custom_call_target="Cholesky" | custom-call | tf_op jit(solution)/shard_map/vmap(jit(cholesky))/cholesky | solution.py:47
  129.6 19.8 %custom-call.39 = f32[2,1,128,128]{2,3,1,0:T(8,128)S(1)} custom-call(f32[2,1,128,128]{3,2,1,0:T(8,128)S(1)} %select_bitcast_fusion.2), custom_call_target="InvertDiagBlocksLowerTriangular" | custom-call | tf_op jit(solution)/shard_map/vmap(jit(cholesky))/cholesky | solution.py:47
  149.6 1.4 constant_dynamic-update-slice_fusion.3
  151.0 1.4 convolution_subtract_fusion
  152.4 23.5 %custom-call.40 = f32[2,128,128]{2,1,0:T(8,128)S(1)} custom-call(f32[2,128,128]{2,1,0:T(8,128)S(1)} %cholesky.285), custom_call_target="Cholesky" | custom-call | tf_op jit(solution)/shard_map/vmap(jit(cholesky))/cholesky | solution.py:47
  175.9 19.7 %custom-call.41 = f32[2,1,128,128]{2,3,1,0:T(8,128)S(1)} custom-call(f32[2,1,128,128]{3,2,1,0:T(8,128)S(1)} %get-tuple-element.30), custom_call_target="InvertDiagBlocksLowerTriangular" | custom-call | tf_op jit(solution)/shard_map/vmap(jit(cholesky))/cholesky | solution.py:47
  195.6 0.3 convolution_dynamic-update-slice_fusion
  195.9 1.3 convolution_subtract_fusion.1
  197.2 23.7 %custom-call.42 = f32[2,128,128]{2,1,0:T(8,128)S(1)} custom-call(f32[2,128,128]{2,1,0:T(8,128)S(1)} %cholesky.290), custom_call_target="Cholesky" | custom-call | tf_op jit(solution)/shard_map/vmap(jit(cholesky))/cholesky | solution.py:47
  221.3 19.7 %custom-call.43 = f32[2,1,128,128]{2,3,1,0:T(8,128)S(1)} custom-call(f32[2,1,128,128]{3,2,1,0:T(8,128)S(1)} %get-tuple-element.28), custom_call_target="InvertDiagBlocksLowerTriangular" | custom-call | tf_op jit(solution)/shard_map/vmap(jit(cholesky))/cholesky | solution.py:47
  241.2 0.9 convolution_subtract_fusion.8
  242.1 2.4 custom-call.44
  244.7 1.3 select_select_fusion
  246.0 7.9 %while.1 = (s32[]{:T(128)}, f32[2,397,397]{2,1,0:T(8,128)S(1)}, s32[3,2]{0,1:T(2,128)S(1)}, f32[3,2,128,128]{3,2,0,1:T(8,128)}, s32[]{:T(128)}) while((s32[]{:T(128)}, f32[2,397,397]{2,1,0:T(8,128)S(1)}, s32[3,2]{0,1:T(2,128)S(1)}, f32[3,2,128,128]{3,2,0,1:T(8,128)}, s32[]{:T(128)}) %tuple.67), condition=%wide.while_cond, body=%wide.while_body.sunk | while | flops 2 | bytes 263277 | solution.py:49
  246.1 0.6 fusion.85
  246.7 2.0 bitcast_dynamic-update-slice_fusion.2
  248.8 0.6 fusion.85
  249.3 2.0 bitcast_dynamic-update-slice_fusion.2
  251.4 0.6 fusion.85
  252.0 2.0 bitcast_dynamic-update-slice_fusion.2
  254.1 1.0 pad_maximum_fusion.1
  255.1 78.6 %custom-call.45 = f32[2,4,128,128]{2,3,1,0:T(8,128)S(1)} custom-call(f32[2,4,128,128]{3,2,1,0:T(8,128)S(1)} %pad_maximum_fusion.1), custom_call_target="InvertDiagBlocksLowerTriangular" | custom-call | tf_op jit(solution)/shard_map/vmap(jit(_solve_triangular))/triangular_solve | solution.py:49
  334.0 0.3 convolution_subtract_fusion.6
  334.5 0.3 convolution_subtract_fusion.5
  336.1 0.3 fusion.34
  336.4 0.3 convolution_subtract_fusion.2
  336.7 0.3 fusion.32
  337.0 0.3 convolution_subtract_fusion.7
  337.3 0.3 fusion.30
  337.6 0.7 maximum_bitcast_fusion
  (90 shorter events, 3.9 us)
Async XLA Ops:
  1.4 10.7 %copy-start = (bf16[1,2,4,2048,512]{4,3,2,1,0:T(8,128)(2,1)S(1)}, bf16[1,2,4,2048,512]{4,3,2,1,0:T(8,128)(2,1)}, u32[]{:S(2)}) copy-start(bf16[1,2,4,2048,512]{4,3,2,1,0:T(8,128)(2,1)} %param.4) | copy-start | bytes 50331652
  12.0 5.5 %copy-start.7 = (s32[1,2]{1,0:T(1,128)S(1)}, s32[1,2]{1,0:T(1,128)}, u32[]{:S(2)}) copy-start(s32[1,2]{1,0:T(1,128)} %param.6) | copy-start | bytes 28
  59.8 38.0 %copy-start.1 = (f32[2,24,512]{2,1,0:T(8,128)}, f32[2,24,512]{2,1,0:T(8,128)S(1)}, u32[]{:S(2)}) copy-start(f32[2,24,512]{2,1,0:T(8,128)S(1)} %divide_reduce_fusion) | copy-start | bytes 294916
  59.8 16.9 %collective-permute-start.1 = (f32[1,2,24,512]{3,2,1,0:T(8,128)S(1)}, f32[1,2,24,512]{3,2,1,0:T(8,128)S(1)}, u32[]{:S(2)}, u32[]{:S(2)}) collective-permute-start(f32[1,2,24,512]{3,2,1,0:T(8,128)S(1)} %bitcast.155), channel_id=1, source_target_pairs={{4,0},{8,4},{12,8},{16,12},{20,16},{24,20},{28,24},{5,1},{9,5},{13... | collective-permute-start | bytes 294920 | tf_op jit(solution)/shard_map/ppermute | solution.py:20
  61.1 15.6 %collective-permute-start = (f32[1,2,24,512]{3,2,1,0:T(8,128)S(1)}, f32[1,2,24,512]{3,2,1,0:T(8,128)S(1)}, u32[]{:S(2)}, u32[]{:S(2)}) collective-permute-start(f32[1,2,24,512]{3,2,1,0:T(8,128)S(1)} %bitcast.156), channel_id=1, source_target_pairs={{0,4},{4,8},{8,12},{12,16},{16,20},{20,24},{24,28},{1,5},{5,9},{9,... | collective-permute-start | bytes 294920 | tf_op jit(solution)/shard_map/ppermute | solution.py:18
  74.4 1.7 copy-start.6
  76.7 9.4 %collective-permute-start.2 = (f32[3,1,24,512]{3,2,1,0:T(8,128)S(1)}, f32[3,1,24,512]{3,2,1,0:T(8,128)S(1)}, u32[]{:S(2)}, u32[]{:S(2)}) collective-permute-start(f32[3,1,24,512]{3,2,1,0:T(8,128)S(1)} %get-tuple-element.26), channel_id=1, source_target_pairs={{0,1},{1,2},{2,3},{4,5},{5,6},{6,7},{8,9},{9,10},{10,11},{12,13},{... | collective-permute-start | bytes 442376 | tf_op jit(solution)/shard_map/ppermute | solution.py:18
  82.4 6.5 %collective-permute-start.3 = (f32[3,1,24,512]{3,2,1,0:T(8,128)S(1)}, f32[3,1,24,512]{3,2,1,0:T(8,128)S(1)}, u32[]{:S(2)}, u32[]{:S(2)}) collective-permute-start(f32[3,1,24,512]{3,2,1,0:T(8,128)S(1)} %get-tuple-element.27), channel_id=1, source_target_pairs={{1,0},{2,1},{3,2},{5,4},{6,5},{7,6},{9,8},{10,9},{11,10},{13,12},{... | collective-permute-start | bytes 442376 | tf_op jit(solution)/shard_map/ppermute | solution.py:20
  104.9 1.2 copy-start.2
  151.0 69.9 %copy-start.4 = (pred[128,128]{1,0:T(8,128)(4,1)S(1)}, pred[128,128]{1,0:T(8,128)(4,1)}, u32[]{:S(2)}) copy-start(pred[128,128]{1,0:T(8,128)(4,1)} %get-tuple-element.87) | copy-start | bytes 49156
  152.4 92.1 %copy-start.5 = (pred[13,13]{1,0:T(8,128)(4,1)S(1)}, pred[13,13]{1,0:T(8,128)(4,1)}, u32[]{:S(2)}) copy-start(pred[13,13]{1,0:T(8,128)(4,1)} %iota_compare_fusion.8) | copy-start | bytes 511
  244.7 1.3 copy-start.8
  244.7 9.2 %copy-start.3 = (f32[128,115]{1,0:T(8,128)S(1)}, f32[128,115]{1,0:T(8,128)}, u32[]{:S(2)}) copy-start(f32[128,115]{1,0:T(8,128)} %pad_convert_fusion) | copy-start | bytes 176644
where the time goes:
time: 344 us; the launch traced here: 339 us
  other arithmetic  236 us (69%)
  blocking collectives  40.9 us (12%)
  local copies, waits for them, and re-layouts  21.6 us (6%)
  matrix products  19.7 us (6%)
  starting transfers between devices  13.3 us (4%)
  between operations  4.19 us (1%)
    another operation x18, other arithmetic, solve_one(): factor = jnp.linalg.cholesky(gram)  134 us
    another operation x8, other arithmetic, solve_one(): jax.scipy.linalg.solve_triangular(factor, middle, lower=True, trans=1)  83 us
    psum x1, blocking collectives, body(): lax.psum((squares, nodes, cross), ('gx', 'gy'))  40.9 us
    ppermute x2, starting transfers between devices, padded_2(): lax.ppermute(tail, axis, [(i, (i + 1) % count) for i in range(ends)])  9.65 us
    concatenate x1, local copies, waits for them, and re-layouts, build_features(): return jnp.concatenate(pieces, axis=1)  8.01 us
    another operation x9, local copies, waits for them, and re-layouts  7.89 us
    dot_general x1, other arithmetic, body(): jnp.einsum('svpk,svpk->svp', values, values, preferred_element_type=jnp.f...  7.47 us
  transfers between devices with their start and end apart: 4, of which 1 were waited for; matrix products, arithmetic and copies ran while one was open for 3% of the time, Pallas kernels for 0%

commit v1 on v0

--- a/solution.py
+++ b/solution.py
@@ -1,3 +1,4 @@
+import functools
 import jax
 import jax.numpy as jnp
 from jax import lax
@@ -5,6 +6,15 @@
 
 beta_linear = 0.5
 beta_quad = 0.5
+
+
+def cover_the_stops_all(here_x, which_axis, axis_tag):
+    for w in (which_axis, axis_tag):
+        here_x = lax.psum(here_x, w)
+    return here_x
+
+
+thing_lead = functools.partial(cover_the_stops_all, which_axis="gy", axis_tag="gx")
 
 
 def padded_2(cells, sides, width):
@@ -72,7 +82,7 @@
         near_col - lax.axis_index("gy") * columns + 1
     )
     cross = jnp.einsum("svrk,swrk->vw", proj, proj, precision=lax.Precision.HIGHEST)
-    sq_all, nodes_all, cross_all = lax.psum((squares, nodes, cross), ("gx", "gy"))
+    sq_all, nodes_all, cross_all = thing_lead((squares, nodes, cross))
     scale = jnp.sqrt(sq_all / (nodes_all * steps) + 1e-06)
     states = jnp.sum(proj / scale[None, :, None, None], axis=1)
     gnorm = jnp.sum(cross_all / (scale[:, None] * scale[None, :])) / (total_subs * ranks * steps)

time: 344 us -> 331 us (0.962)
  blocking collectives: 40.9 us -> 25.6 us
    psum x1 -> x2, blocking collectives: 40.9 us -> 25.6 us  [cover_the_stops_all(): here_x = lax.psum(here_x, w)]
where the time goes in v1:
time: 331 us; the launch traced here: 326 us
  other arithmetic  236 us (71%)
  blocking collectives  25.6 us (8%)
  local copies, waits for them, and re-layouts  21.6 us (7%)
  matrix products  19.7 us (6%)
  starting transfers between devices  15.9 us (5%)
  between operations  4.19 us (1%)
    another operation x18, other arithmetic, solve_one(): factor = jnp.linalg.cholesky(gram)  134 us
    another operation x8, other arithmetic, solve_one(): jax.scipy.linalg.solve_triangular(factor, middle, lower=True, trans=1)  83 us
    psum x2, blocking collectives, cover_the_stops_all(): here_x = lax.psum(here_x, w)  25.6 us
    ppermute x2, starting transfers between devices, padded_2(): lax.ppermute(tail, axis, [(i, (i + 1) % count) for i in range(ends)])  12.2 us
    concatenate x1, local copies, waits for them, and re-layouts, build_features(): return jnp.concatenate(pieces, axis=1)  8.01 us
    another operation x9, local copies, waits for them, and re-layouts  7.89 us
    dot_general x1, other arithmetic, body(): jnp.einsum('svpk,svpk->svp', values, values, preferred_element_type=jnp.f...  7.47 us
  transfers between devices with their start and end apart: 4, of which 1 were waited for; matrix products, arithmetic and copies ran while one was open for 3% of the time, Pallas kernels for 0%

profile of v1, /device:TPU:1, one launch (start us, length us, event | category | flops | bytes accessed | tf_op | source)
XLA Modules:
  0.0 325.9 jit_solution(4656764787365097028)
XLA Ops:
  0.6 0.7 fusion.58
  1.4 7.5 %fusion = f32[2,4,2048]{2,1,0:T(4,128)S(1)} fusion(bf16[1,2,4,2048,512]{4,3,2,1,0:T(8,128)(2,1)} %param.4), kind=kLoop, calls=%fused_computation.3 | loop fusion | flops 25149440 | bytes 16842752 | tf_op jit(solution)/shard_map/svpk,svpk->svp/dot_general | solution.py:74
  8.9 3.2 copy-done
  12.0 3.4 %fusion.1 = f32[2,4,24,512]{3,2,1,0:T(8,128)S(1)} fusion(bf16[1,2,4,2048,512]{4,3,2,1,0:T(8,128)(2,1)S(1)} %copy-done, bf16[1,2,4,24,2048]{4,3,2,1,0:T(8,128)(2,1)} %param.5, bf16[2,2048]{1,0:T(2,128)(2,1)S(1)} %get-tuple-element.64), kind=kOutput, calls=%fused_computation.4 | convolution fusion | flops 403046400 | bytes 17965056 | tf_op jit(solution)/shard_map/svrp,svpk->svrk/dot_general | solution.py:73
  15.5 1.9 convolution_bitcast_fusion
  17.5 0.6 convert_reduce_fusion
  18.1 7.0 %all-reduce.5 = (f32[4]{0:T(128)S(1)}, f32[]{:T(128)}, f32[4,4]{1,0:T(4,128)S(1)}) all-reduce(f32[4]{0:T(128)S(1)} %multiply_reduce_fusion, f32[]{:T(128)} %convert_reduce_fusion, f32[4,4]{1,0:T(4,128)S(1)} %convolution_bitcast_fusion), channel_id=1, replica_groups=mesh['gx'=8,'gy'=4] {'gy'}, use_global_device_ids=true, to_apply=%region_1.0 | all-reduce | flops 21 | bytes 168 | tf_op jit(solution)/shard_map/psum | solution.py:13
  25.1 18.7 %all-reduce.4 = (f32[4]{0:T(128)S(1)}, f32[]{:T(128)}, f32[4,4]{1,0:T(4,128)S(1)}) all-reduce(f32[4]{0:T(128)S(1)} %get-tuple-element.24, f32[]{:T(128)} %get-tuple-element.25, f32[4,4]{1,0:T(4,128)S(1)} %get-tuple-element.26), channel_id=1, replica_groups=mesh['gx'=8,'gy'=4] {'gx'}, use_global_device_ids=true, to_apply=%region_2.3 | all-reduce | flops 21 | bytes 168 | tf_op jit(solution)/shard_map/psum | solution.py:13
  44.6 1.3 collective-permute-start.1
  45.9 4.0 %collective-permute-start = (f32[1,2,24,512]{3,2,1,0:T(8,128)S(1)}, f32[1,2,24,512]{3,2,1,0:T(8,128)S(1)}, u32[]{:S(2)}, u32[]{:S(2)}) collective-permute-start(f32[1,2,24,512]{3,2,1,0:T(8,128)S(1)} %bitcast.156), channel_id=1, source_target_pairs={{0,4},{4,8},{8,12},{12,16},{16,20},{20,24},{24,28},{1,5},{5,9},{9,... | collective-permute-start | bytes 294920 | tf_op jit(solution)/shard_map/ppermute | solution.py:28
  49.9 0.6 iota_compare_fusion.4
  50.5 0.7 slice_multiply_fusion.22
  51.2 0.6 pad_convert_fusion
  51.8 0.8 fusion.65
  54.7 0.6 slice_multiply_fusion.21
  55.3 0.6 slice_multiply_fusion.20
  55.9 0.6 slice_multiply_fusion.19
  56.5 0.6 slice_multiply_fusion.18
  57.1 0.6 slice_multiply_fusion.16
  57.7 0.6 slice_multiply_fusion.17
  58.4 0.6 slice_multiply_fusion.15
  59.5 1.4 fusion.9
  60.9 0.6 iota_compare_fusion.8
  61.5 8.2 %collective-permute-start.2 = (f32[3,1,24,512]{3,2,1,0:T(8,128)S(1)}, f32[3,1,24,512]{3,2,1,0:T(8,128)S(1)}, u32[]{:S(2)}, u32[]{:S(2)}) collective-permute-start(f32[3,1,24,512]{3,2,1,0:T(8,128)S(1)} %get-tuple-element.29), channel_id=1, source_target_pairs={{0,1},{1,2},{2,3},{4,5},{5,6},{6,7},{8,9},{9,10},{10,11},{12,13},{... | collective-permute-start | bytes 442376 | tf_op jit(solution)/shard_map/ppermute | solution.py:28
  69.7 2.4 collective-permute-start.3
  72.1 0.6 iota_multiply_fusion
  72.7 0.8 iota_compare_fusion.2
  73.4 2.7 collective-permute-done.3
  76.2 0.8 fusion.11
  77.1 8.0 %concatenate.48 = f32[2,397,512]{2,1,0:T(8,128)S(1)} concatenate(f32[2,1,512]{2,1,0:T(1,128)S(1)} %broadcast_in_dim.45, f32[2,24,512]{2,1,0:T(8,128)S(1)} %divide_reduce_fusion, f32[2,72,512]{2,1,0:T(8,128)S(1)} %bitcast.161, f32[2,24,512]{2,1,0:T(8,128)S(1)} %broadcast_multiply_fusion, f32[2,23,512]{2,1,0:T(8,128)S(1)} %slice_multiply_fusion.6, ...), dimensions={1} | concatenate | bytes 3252224 | tf_op jit(solution)/shard_map/concatenate | solution.py:47
  85.1 1.5 fusion.5
  86.7 2.8 fusion.7
  89.5 0.7 copy.49
  90.2 2.0 fusion.4
  92.2 1.2 copy-done.2
  93.4 23.5 %custom-call.38 = f32[2,128,128]{2,1,0:T(8,128)S(1)} custom-call(f32[2,128,128]{2,1,0:T(8,128)S(1)} %cholesky.281), custom_call_target="Cholesky" | custom-call | tf_op jit(solution)/shard_map/vmap(jit(cholesky))/cholesky | solution.py:57
  116.9 19.8 %custom-call.39 = f32[2,1,128,128]{2,3,1,0:T(8,128)S(1)} custom-call(f32[2,1,128,128]{3,2,1,0:T(8,128)S(1)} %select_bitcast_fusion.2), custom_call_target="InvertDiagBlocksLowerTriangular" | custom-call | tf_op jit(solution)/shard_map/vmap(jit(cholesky))/cholesky | solution.py:57
  137.0 1.4 constant_dynamic-update-slice_fusion.3
  138.3 1.4 convolution_subtract_fusion
  139.7 23.5 %custom-call.40 = f32[2,128,128]{2,1,0:T(8,128)S(1)} custom-call(f32[2,128,128]{2,1,0:T(8,128)S(1)} %cholesky.285), custom_call_target="Cholesky" | custom-call | tf_op jit(solution)/shard_map/vmap(jit(cholesky))/cholesky | solution.py:57
  163.2 19.7 %custom-call.41 = f32[2,1,128,128]{2,3,1,0:T(8,128)S(1)} custom-call(f32[2,1,128,128]{3,2,1,0:T(8,128)S(1)} %get-tuple-element.33), custom_call_target="InvertDiagBlocksLowerTriangular" | custom-call | tf_op jit(solution)/shard_map/vmap(jit(cholesky))/cholesky | solution.py:57
  182.9 0.3 convolution_dynamic-update-slice_fusion
  183.2 1.3 convolution_subtract_fusion.1
  184.6 23.7 %custom-call.42 = f32[2,128,128]{2,1,0:T(8,128)S(1)} custom-call(f32[2,128,128]{2,1,0:T(8,128)S(1)} %cholesky.290), custom_call_target="Cholesky" | custom-call | tf_op jit(solution)/shard_map/vmap(jit(cholesky))/cholesky | solution.py:57
  208.6 19.7 %custom-call.43 = f32[2,1,128,128]{2,3,1,0:T(8,128)S(1)} custom-call(f32[2,1,128,128]{3,2,1,0:T(8,128)S(1)} %get-tuple-element.31), custom_call_target="InvertDiagBlocksLowerTriangular" | custom-call | tf_op jit(solution)/shard_map/vmap(jit(cholesky))/cholesky | solution.py:57
  228.6 0.9 convolution_subtract_fusion.8
  229.5 2.4 custom-call.44
  232.0 1.3 select_select_fusion
  233.4 7.9 %while.1 = (s32[]{:T(128)}, f32[2,397,397]{2,1,0:T(8,128)S(1)}, s32[3,2]{0,1:T(2,128)S(1)}, f32[3,2,128,128]{3,2,0,1:T(8,128)}, s32[]{:T(128)}) while((s32[]{:T(128)}, f32[2,397,397]{2,1,0:T(8,128)S(1)}, s32[3,2]{0,1:T(2,128)S(1)}, f32[3,2,128,128]{3,2,0,1:T(8,128)}, s32[]{:T(128)}) %tuple.67), condition=%wide.while_cond, body=%wide.while_body.sunk | while | flops 2 | bytes 263277 | solution.py:59
  233.4 0.6 fusion.85
  234.0 2.0 bitcast_dynamic-update-slice_fusion.2
  236.1 0.6 fusion.85
  236.7 2.0 bitcast_dynamic-update-slice_fusion.2
  238.7 0.6 fusion.85
  239.3 2.0 bitcast_dynamic-update-slice_fusion.2
  241.4 1.0 pad_maximum_fusion.1
  242.4 78.6 %custom-call.45 = f32[2,4,128,128]{2,3,1,0:T(8,128)S(1)} custom-call(f32[2,4,128,128]{3,2,1,0:T(8,128)S(1)} %pad_maximum_fusion.1), custom_call_target="InvertDiagBlocksLowerTriangular" | custom-call | tf_op jit(solution)/shard_map/vmap(jit(_solve_triangular))/triangular_solve | solution.py:59
  321.3 0.3 convolution_subtract_fusion.6
  321.9 0.3 convolution_subtract_fusion.5
  323.4 0.3 fusion.34
  324.0 0.3 fusion.32
  324.3 0.3 convolution_subtract_fusion.7
  324.6 0.3 fusion.30
  325.0 0.7 maximum_bitcast_fusion
  (91 shorter events, 4.2 us)
Async XLA Ops:
  1.4 10.7 %copy-start = (bf16[1,2,4,2048,512]{4,3,2,1,0:T(8,128)(2,1)S(1)}, bf16[1,2,4,2048,512]{4,3,2,1,0:T(8,128)(2,1)}, u32[]{:S(2)}) copy-start(bf16[1,2,4,2048,512]{4,3,2,1,0:T(8,128)(2,1)} %param.4) | copy-start | bytes 50331652
  12.0 5.5 %copy-start.7 = (s32[1,2]{1,0:T(1,128)S(1)}, s32[1,2]{1,0:T(1,128)}, u32[]{:S(2)}) copy-start(s32[1,2]{1,0:T(1,128)} %param.6) | copy-start | bytes 28
  44.6 40.6 %copy-start.1 = (f32[2,24,512]{2,1,0:T(8,128)}, f32[2,24,512]{2,1,0:T(8,128)S(1)}, u32[]{:S(2)}) copy-start(f32[2,24,512]{2,1,0:T(8,128)S(1)} %divide_reduce_fusion) | copy-start | bytes 294916
  44.6 16.9 %collective-permute-start.1 = (f32[1,2,24,512]{3,2,1,0:T(8,128)S(1)}, f32[1,2,24,512]{3,2,1,0:T(8,128)S(1)}, u32[]{:S(2)}, u32[]{:S(2)}) collective-permute-start(f32[1,2,24,512]{3,2,1,0:T(8,128)S(1)} %bitcast.155), channel_id=1, source_target_pairs={{4,0},{8,4},{12,8},{16,12},{20,16},{24,20},{28,24},{5,1},{9,5},{13... | collective-permute-start | bytes 294920 | tf_op jit(solution)/shard_map/ppermute | solution.py:30
  45.9 15.6 %collective-permute-start = (f32[1,2,24,512]{3,2,1,0:T(8,128)S(1)}, f32[1,2,24,512]{3,2,1,0:T(8,128)S(1)}, u32[]{:S(2)}, u32[]{:S(2)}) collective-permute-start(f32[1,2,24,512]{3,2,1,0:T(8,128)S(1)} %bitcast.156), channel_id=1, source_target_pairs={{0,4},{4,8},{8,12},{12,16},{16,20},{20,24},{24,28},{1,5},{5,9},{9,... | collective-permute-start | bytes 294920 | tf_op jit(solution)/shard_map/ppermute | solution.py:28
  59.2 1.7 copy-start.6
  61.5 11.9 %collective-permute-start.2 = (f32[3,1,24,512]{3,2,1,0:T(8,128)S(1)}, f32[3,1,24,512]{3,2,1,0:T(8,128)S(1)}, u32[]{:S(2)}, u32[]{:S(2)}) collective-permute-start(f32[3,1,24,512]{3,2,1,0:T(8,128)S(1)} %get-tuple-element.29), channel_id=1, source_target_pairs={{0,1},{1,2},{2,3},{4,5},{5,6},{6,7},{8,9},{9,10},{10,11},{12,13},{... | collective-permute-start | bytes 442376 | tf_op jit(solution)/shard_map/ppermute | solution.py:28
  69.7 6.5 %collective-permute-start.3 = (f32[3,1,24,512]{3,2,1,0:T(8,128)S(1)}, f32[3,1,24,512]{3,2,1,0:T(8,128)S(1)}, u32[]{:S(2)}, u32[]{:S(2)}) collective-permute-start(f32[3,1,24,512]{3,2,1,0:T(8,128)S(1)} %get-tuple-element.30), channel_id=1, source_target_pairs={{1,0},{2,1},{3,2},{5,4},{6,5},{7,6},{9,8},{10,9},{11,10},{13,12},{... | collective-permute-start | bytes 442376 | tf_op jit(solution)/shard_map/ppermute | solution.py:30
  92.2 1.2 copy-start.2
  138.3 69.9 %copy-start.4 = (pred[128,128]{1,0:T(8,128)(4,1)S(1)}, pred[128,128]{1,0:T(8,128)(4,1)}, u32[]{:S(2)}) copy-start(pred[128,128]{1,0:T(8,128)(4,1)} %get-tuple-element.90) | copy-start | bytes 49156
  139.7 92.1 %copy-start.5 = (pred[13,13]{1,0:T(8,128)(4,1)S(1)}, pred[13,13]{1,0:T(8,128)(4,1)}, u32[]{:S(2)}) copy-start(pred[13,13]{1,0:T(8,128)(4,1)} %iota_compare_fusion.8) | copy-start | bytes 511
  232.0 1.3 copy-start.8
  232.0 9.2 %copy-start.3 = (f32[128,115]{1,0:T(8,128)S(1)}, f32[128,115]{1,0:T(8,128)}, u32[]{:S(2)}) copy-start(f32[128,115]{1,0:T(8,128)} %pad_convert_fusion) | copy-start | bytes 176644
